TPU v7x, 32 devices: a whole 2x2x4 slice. The times are simulated.
32 devices in a mesh: groups: 2 (over y), ep: 4 (over z), tp: 2 (over x), dp: 2 (over core).
Axes of the slice: x: 2, y: 2, z: 4, core: 2. Of those that a mesh axis runs over, the one named last changes fastest.
Arguments:
- tokens: bfloat16 [256, 5120], P(('groups', 'ep', 'tp', 'dp')), parts along dimension 0, may hold values from -6 to 6
- route_weights: float32 [256, 8], P(('groups', 'ep', 'tp', 'dp')), parts along dimension 0, may hold values from 0.1 to 1
- expert_ids: int32 [256, 8], P(('groups', 'ep', 'tp', 'dp')), parts along dimension 0, may hold values from 0 to 31, all different within a row; in each aligned block of 8 rows (0 to 7, 8 to 15, ...) at most 4 rows name the same one
- gate_weight: bfloat16 [32, 5120, 1024], P('ep', None, ('tp', 'dp')), may hold values from -0.078125 to 0.078125
- up_weight: bfloat16 [32, 5120, 1024], P('ep', None, ('tp', 'dp')), may hold values from -0.078125 to 0.078125
- down_weight: bfloat16 [32, 1024, 5120], P('ep', None, ('tp', 'dp')), may hold values from -0.1875 to 0.1875
Outputs:
- combined: bfloat16 [256, 5120], P(('groups', 'ep', 'tp', 'dp')), parts along dimension 0
There are 2 independent parts, one for each index of `groups`. A program takes and returns all parts, laid end to end along the dimension named above; an argument that names none is the same for every part. Nothing has to cross between parts.
Inputs may be any that keep to these rules, and one draw needn't show every extreme that they name: `expert_ids`: each row names 8 different experts. Among the 8 rows of one device no expert is named more than 4 times, and in every draw some device's rows name some expert exactly 4 times.
All inputs are finite; a program needn't handle non-finite values.
Results may differ from a plain program's by a relative error of at most 0.0057.
Values may be sent and summed in bfloat16 or wider, within the bound.
No kernel may reach another device: no remote copies, remote signals or barrier semaphores. Data moves between devices by JAX's collectives and lax.ppermute only.
A program may use at most 128 MiB of HBM per device.

v0:
```python
import jax
import jax.numpy as jnp
from jax import lax
from jax.sharding import PartitionSpec as P

CAP = 4


def route_table(ids, experts, capacity):
    tok_count, top_count = ids.shape
    flat = ids.reshape(-1)
    onehot = (flat[:, None] == jnp.arange(experts, dtype=jnp.int32)[None, :]).astype(jnp.int32)
    slots = jnp.sum(onehot * jnp.cumsum(onehot, axis=0), axis=1) - 1
    place = flat * capacity + slots
    owner = jnp.arange(tok_count * top_count, dtype=jnp.int32) // top_count
    table = jnp.full((experts * capacity,), tok_count, jnp.int32).at[place].set(owner)
    return (place, table)


def per_device(tokens, route_weights, expert_ids, gate_weight, up_weight, down_weight):
    n_owner = lax.axis_size("ep")
    tok_count, top_count = expert_ids.shape
    exp_local = gate_weight.shape[0]
    experts = exp_local * n_owner
    width = tokens.shape[1]
    place, table = route_table(expert_ids, experts, CAP)
    sendbuf = jnp.take(tokens, table, axis=0, mode="fill", fill_value=0).reshape(
        experts, CAP, width
    )
    arrived = lax.all_to_all(sendbuf, "ep", split_axis=0, concat_axis=0, tiled=True)
    arrived = arrived.reshape(1, n_owner, exp_local, CAP, width)
    piece = lax.all_gather(arrived, ("tp", "dp"), axis=0, tiled=True)
    gate = jnp.einsum("gsecd,edf->gsecf", piece, gate_weight, preferred_element_type=jnp.float32)
    up = jnp.einsum("gsecd,edf->gsecf", piece, up_weight, preferred_element_type=jnp.float32)
    hidden = (jax.nn.silu(gate) * up).astype(jnp.bfloat16)
    partial_out = jnp.einsum(
        "gsecf,efd->gsecd",
        lax.all_gather(hidden, ("tp", "dp"), axis=4, tiled=True),
        down_weight,
        preferred_element_type=jnp.float32,
    )
    expert_out = partial_out.astype(jnp.bfloat16)
    mine = lax.all_to_all(expert_out, ("tp", "dp"), split_axis=0, concat_axis=4, tiled=True)
    mine = mine.reshape(n_owner * exp_local, CAP, width)
    returned = lax.all_to_all(mine, "ep", split_axis=0, concat_axis=0, tiled=True)
    picked = jnp.take(returned.reshape(experts * CAP, width), place, axis=0)
    picked = picked.reshape(tok_count, top_count, width).astype(jnp.float32)
    combined = jnp.sum(picked * route_weights[:, :, None], axis=1)
    return combined.astype(jnp.bfloat16)


def solution(mesh):
    return jax.shard_map(
        per_device,
        mesh=mesh,
        in_specs=(
            P(("groups", "ep", "tp", "dp"), None),
            P(("groups", "ep", "tp", "dp"), None),
            P(("groups", "ep", "tp", "dp"), None),
            P("ep", None, ("tp", "dp")),
            P("ep", None, ("tp", "dp")),
            P("ep", None, ("tp", "dp")),
        ),
        out_specs=P(("groups", "ep", "tp", "dp"), None),
        check_vma=False,
    )
```

profile of v0, /device:TPU:0, one launch (start us, length us, event | category | flops | bytes accessed | tf_op | source)
XLA Modules:
  0.0 212.0 jit_solution(12040743795864728024)
XLA Ops:
  6.5 0.8 reshape.76
  7.3 0.7 broadcast_multiply_fusion
  8.0 0.1 fusion.24
  8.1 0.1 reduce_window_sum.11
  8.2 0.2 select_reduce_fusion
  8.4 0.1 mul.40
  8.5 0.8 scatter_custom_fusion
  9.3 1.3 gather_fusion
  10.6 0.5 gather.13
  11.1 0.1 broadcast_in_dim.32
  11.3 0.7 broadcast_select_fusion
  11.9 37.5 %all_to_all.25 = bf16[32,4,5120]{2,1,0:T(4,128)(2,1)S(1)} all-to-all(bf16[32,4,5120]{2,1,0:T(4,128)(2,1)S(1)} %broadcast_select_fusion), channel_id=1, replica_groups=mesh['groups'=2,'ep'=4,'tp'=2,'dp'=2] {'ep'}, dimensions={0} | all-to-all | bytes 2621440 | tf_op jit(solution)/shard_map/all_to_all | solution.py:30
  49.4 1.7 copy.13
  51.1 0.0 all-gather.3.cloned.1.call-update
  51.1 0.2 all-gather.5.cloned.1.call-start
  51.3 39.5 %all-gather.3.cloned.1.call-done = bf16[4,4,8,4,5120]{4,3,1,0,2:T(4,128)(2,1)} async-done(((bf16[1,4,8,4,5120]{4,3,1,0,2:T(4,128)(2,1)}), bf16[4,4,8,4,5120]{4,3,1,0,2:T(4,128)(2,1)}) %all-gather.3.cloned.1.call-update) | async-done | bytes 5242896 | tf_op jit(solution)/shard_map/all_gather | solution.py:32
  90.8 13.1 %fusion.12 = f32[4,4,8,4,256]{4,3,1,0,2:T(4,128)S(1)} fusion(bf16[4,4,8,4,5120]{4,3,1,0,2:T(4,128)(2,1)} %all-gather.3.cloned.1.call-done, bf16[8,5120,256]{2,1,0:T(8,128)(2,1)} %param.9), kind=kOutput, calls=%fused_computation.13 | convolution fusion | flops 1342177280 | bytes 26738688 | tf_op jit(solution)/shard_map/gsecd,edf->gsecf/dot_general | solution.py:33
  103.9 12.2 %fusion.21 = bf16[4,4,8,4,256]{4,3,1,0,2:T(4,128)(2,1)} fusion(bf16[4,4,8,4,5120]{4,3,1,0,2:T(4,128)(2,1)S(1)} %copy-done.4, bf16[8,5120,256]{2,1,0:T(8,128)(2,1)} %param.10, f32[4,4,8,4,256]{4,3,1,0,2:T(4,128)S(1)} %fusion.12), kind=kOutput, calls=%fused_computation.16 | convolution fusion | flops 1342963712 | bytes 27000832 | tf_op jit(solution)/shard_map/gsecd,edf->gsecf/dot_general | solution.py:34
  116.1 0.0 all-gather.5.cloned.1.call-update
  116.1 17.0 %all-gather.5.cloned.1.call-done = bf16[4,4,8,4,1024]{4,3,1,0,2:T(4,128)(2,1)} async-done(((bf16[4,4,8,4,256]{4,3,1,0,2:T(4,128)(2,1)}), bf16[4,4,8,4,1024]{4,3,1,0,2:T(4,128)(2,1)}) %all-gather.5.cloned.1.call-update) | async-done | bytes 1048592 | tf_op jit(solution)/shard_map/all_gather | solution.py:38
  133.1 11.3 %fusion.9 = bf16[4,4,8,4,1280]{4,3,1,0,2:T(4,128)(2,1)S(1)} fusion(bf16[4,4,8,4,1024]{4,3,1,0,2:T(4,128)(2,1)} %all-gather.5.cloned.1.call-done, bf16[8,1024,1280]{2,1,0:T(8,128)(2,1)} %param.11), kind=kOutput, calls=%fused_computation.10 | convolution fusion | flops 1342832640 | bytes 23330816 | tf_op jit(solution)/shard_map/gsecf,efd->gsecd/dot_general | solution.py:36
  144.4 0.5 copy.14
  144.9 19.7 %all_to_all.26 = bf16[4,4,8,4,1280]{4,3,1,2,0:T(4,128)(2,1)S(1)} all-to-all(bf16[4,4,8,4,1280]{4,3,1,2,0:T(4,128)(2,1)S(1)} %copy.14), channel_id=1, replica_groups=mesh['groups'=2,'ep'=4,'tp'=2,'dp'=2] {'tp','dp'}, dimensions={0} | all-to-all | bytes 2621440 | tf_op jit(solution)/shard_map/all_to_all | solution.py:43
  164.6 1.0 copy.22
  165.6 1.4 reshape.108
  167.0 4.7 %all-to-all-start.2 = ((bf16[32,4,5120]{2,1,0:T(4,128)(2,1)}), bf16[32,4,5120]{2,1,0:T(4,128)(2,1)S(1)}, u32[]{:S(2)}, u32[]{:S(2)}) async-start(bf16[32,4,5120]{2,1,0:T(4,128)(2,1)} %reshape.108), calls=%async_computation.2 | async-start | bytes 2621440 | tf_op jit(solution)/shard_map/all_to_all | solution.py:45
  171.7 0.1 sub.15
  171.8 30.9 %all-to-all-done.2 = bf16[32,4,5120]{2,1,0:T(4,128)(2,1)S(1)} async-done(((bf16[32,4,5120]{2,1,0:T(4,128)(2,1)}), bf16[32,4,5120]{2,1,0:T(4,128)(2,1)S(1)}, u32[]{:S(2)}, u32[]{:S(2)}) %all-to-all-start.2) | async-done | bytes 1310752 | tf_op jit(solution)/shard_map/all_to_all | solution.py:45
  202.7 0.3 reshape.79
  203.0 0.0 copy-start.3
  203.0 0.9 gather_fusion.1
  204.0 1.2 multiply_reduce_fusion
  (18 shorter events, 0.1 us)
Async XLA Ops:
  6.5 2.8 %copy-start = (bf16[8,5120]{1,0:T(8,128)(2,1)S(1)}, bf16[8,5120]{1,0:T(8,128)(2,1)}, u32[]{:S(2)}) copy-start(bf16[8,5120]{1,0:T(8,128)(2,1)} %param.6) | copy-start | bytes 245764
  6.5 84.3 %all-gather.3.cloned.1.call-start = ((), (), s32[]{:S(2)}) async-start(), calls=%async_computation.3 | async-start | bytes 6553600 | tf_op jit(solution)/shard_map/all_gather | solution.py:32
  51.1 82.0 %all-gather.5.cloned.1.call-start = ((), (), s32[]{:S(2)}) async-start(), calls=%async_computation.4 | async-start | bytes 1310720 | tf_op jit(solution)/shard_map/all_gather | solution.py:38
  90.8 13.1 %copy-start.4 = (bf16[4,4,8,4,5120]{4,3,1,0,2:T(4,128)(2,1)S(1)}, bf16[4,4,8,4,5120]{4,3,1,0,2:T(4,128)(2,1)}, u32[]{:S(2)}) copy-start(bf16[4,4,8,4,5120]{4,3,1,0,2:T(4,128)(2,1)} %all-gather.3.cloned.1.call-done) | copy-start | bytes 15728644
  167.0 4.8 %copy-start.2 = (s32[8,8]{1,0:T(8,128)S(1)}, s32[8,8]{1,0:T(8,128)}, u32[]{:S(2)}) copy-start(s32[8,8]{1,0:T(8,128)} %param.8) | copy-start | bytes 772
  167.0 35.7 %all-to-all-start.2 = ((bf16[32,4,5120]{2,1,0:T(4,128)(2,1)}), bf16[32,4,5120]{2,1,0:T(4,128)(2,1)S(1)}, u32[]{:S(2)}, u32[]{:S(2)}) async-start(bf16[32,4,5120]{2,1,0:T(4,128)(2,1)} %reshape.108), calls=%async_computation.2 | async-start | bytes 2621440 | tf_op jit(solution)/shard_map/all_to_all | solution.py:45
  203.0 1.0 copy-start.3
  203.0 2.1 %copy-start.1 = (bf16[8,5120]{1,0:T(8,128)(2,1)S(1)}, bf16[8,5120]{1,0:T(8,128)(2,1)}, u32[]{:S(2)}) copy-start(bf16[8,5120]{1,0:T(8,128)(2,1)} %param.6) | copy-start | bytes 245764
Sparse Core Ops, SparseCore 0:
  51.2 39.5 all-gather.2
  116.2 16.8 all-gather.4
where the time goes:
time: 212 us
  waiting for transfers between devices  87.3 us (41%)
  blocking collectives  57.2 us (27%)
  matrix products  36.6 us (17%)
  between operations  13.6 us (6%)
  local copies, waits for them, and re-layouts  9.45 us (4%)
  starting transfers between devices  4.95 us (2%)
  other arithmetic  2.91 us (1%)
    all_gather x1, waiting for transfers between devices, per_device(): piece = lax.all_gather(arrived, ('tp', 'dp'), axis=0, tiled=True)  39.5 us
    all_to_all x1, blocking collectives, per_device(): lax.all_to_all(sendbuf, 'ep', split_axis=0, concat_axis=0, tiled=True)  37.5 us
    all_to_all x1, waiting for transfers between devices, per_device(): lax.all_to_all(mine, 'ep', split_axis=0, concat_axis=0, tiled=True)  30.9 us
    all_to_all x1, blocking collectives, per_device(): lax.all_to_all(expert_out, ('tp', 'dp'), split_axis=0, concat_axis=4, til...  19.7 us
    all_gather x1, waiting for transfers between devices, per_device(): lax.all_gather(hidden, ('tp', 'dp'), axis=4, tiled=True)  17 us
    dot_general x1, matrix products, per_device(): jnp.einsum('gsecd,edf->gsecf', piece, gate_weight, preferred_element_type...  13.1 us
    dot_general x1, matrix products, per_device(): jnp.einsum('gsecd,edf->gsecf', piece, up_weight, preferred_element_type=j...  12.2 us
    dot_general x1, matrix products, per_device(): jnp.einsum('gsecf,efd->gsecd', lax.all_gather(hidden, ('tp', 'dp'), axis=...  11.3 us
  transfers between devices with their start and end apart: 3, of which 3 were waited for; matrix products, arithmetic and copies ran while one was open for 0% of the time, Pallas kernels for 0%

commit v1 on v0

--- a/solution.py
+++ b/solution.py
@@ -4,6 +4,18 @@
 from jax.sharding import PartitionSpec as P
 
 CAP = 4
+
+
+def product_in_turn(shard, axis, dim, term):
+    size, index = (lax.axis_size(axis), lax.axis_index(axis))
+    downward = [(i, (i - 1) % size) for i in range(size)]
+    width = shard.shape[dim]
+    held = shard
+    subtotal = term(held, index * width)
+    for step in range(1, size):
+        held = lax.ppermute(held, axis, downward)
+        subtotal = subtotal + term(held, (index + step) % size * width)
+    return subtotal
 
 
 def route_table(ids, experts, capacity):
@@ -33,11 +45,16 @@
     gate = jnp.einsum("gsecd,edf->gsecf", piece, gate_weight, preferred_element_type=jnp.float32)
     up = jnp.einsum("gsecd,edf->gsecf", piece, up_weight, preferred_element_type=jnp.float32)
     hidden = (jax.nn.silu(gate) * up).astype(jnp.bfloat16)
-    partial_out = jnp.einsum(
-        "gsecf,efd->gsecd",
-        lax.all_gather(hidden, ("tp", "dp"), axis=4, tiled=True),
-        down_weight,
-        preferred_element_type=jnp.float32,
+    partial_out = product_in_turn(
+        hidden,
+        ("tp", "dp"),
+        4,
+        lambda part, at: jnp.einsum(
+            "gsecf,efd->gsecd",
+            part,
+            lax.dynamic_slice_in_dim(down_weight, at, part.shape[4], axis=1),
+            preferred_element_type=jnp.float32,
+        ),
     )
     expert_out = partial_out.astype(jnp.bfloat16)
     mine = lax.all_to_all(expert_out, ("tp", "dp"), split_axis=0, concat_axis=4, tiled=True)

time: 212 us -> 204 us (0.962)
  waiting for transfers between devices: 87.3 us -> 70.5 us
  matrix products: 36.6 us -> 43.3 us
    all_gather x1 -> x0, waiting for transfers between devices: 17 us -> none  [per_device(): lax.all_gather(hidden, ('tp', 'dp'), axis=4, tiled=True)]
    dot_general x1 -> x4, matrix products: 11.3 us -> 18.8 us  [per_device(): jnp.einsum('gsecf,efd->gsecd', part, lax.dynamic_slice_in_dim(down_weight...]
    ppermute x0 -> x3, starting transfers between devices: none -> 2.27 us  [product_in_turn(): held = lax.ppermute(held, axis, downward)]
  transfers between devices with their start and end apart: 3 -> 5, of which waited for: 3 -> 2; matrix products, arithmetic and copies ran while one was open for 0% -> 8% of each run, Pallas kernels for 0% -> 0%
where the time goes in v1:
time: 204 us
  waiting for transfers between devices  70.5 us (35%)
  blocking collectives  57.3 us (28%)
  matrix products  43.3 us (21%)
  between operations  13.6 us (7%)
  local copies, waits for them, and re-layouts  9.42 us (5%)
  starting transfers between devices  6.86 us (3%)
  other arithmetic  2.94 us (1%)
    all_gather x1, waiting for transfers between devices, per_device(): piece = lax.all_gather(arrived, ('tp', 'dp'), axis=0, tiled=True)  39.7 us
    all_to_all x1, blocking collectives, per_device(): lax.all_to_all(sendbuf, 'ep', split_axis=0, concat_axis=0, tiled=True)  37.5 us
    all_to_all x1, waiting for transfers between devices, per_device(): lax.all_to_all(mine, 'ep', split_axis=0, concat_axis=0, tiled=True)  30.9 us
    all_to_all x1, blocking collectives, per_device(): lax.all_to_all(expert_out, ('tp', 'dp'), split_axis=0, concat_axis=4, til...  19.8 us
    dot_general x4, matrix products, per_device(): jnp.einsum('gsecf,efd->gsecd', part, lax.dynamic_slice_in_dim(down_weight...  18.8 us
    dot_general x1, matrix products, per_device(): jnp.einsum('gsecd,edf->gsecf', piece, gate_weight, preferred_element_type...  13.1 us
    dot_general x1, matrix products, per_device(): jnp.einsum('gsecd,edf->gsecf', piece, up_weight, preferred_element_type=j...  11.5 us
    all_to_all x1, starting transfers between devices, per_device(): lax.all_to_all(mine, 'ep', split_axis=0, concat_axis=0, tiled=True)  4.59 us
  transfers between devices with their start and end apart: 5, of which 2 were waited for; matrix products, arithmetic and copies ran while one was open for 8% of the time, Pallas kernels for 0%

profile of v1, /device:TPU:0, one launch (start us, length us, event | category | flops | bytes accessed | tf_op | source)
XLA Modules:
  0.0 204.0 jit_solution(1387919113791989825)
XLA Ops:
  6.5 0.7 broadcast_multiply_fusion
  7.3 0.8 reshape.76
  8.0 0.1 mul.57
  8.2 0.1 reduce_window_sum.11
  8.3 0.2 select_reduce_fusion
  8.5 0.8 scatter_custom_fusion
  9.3 1.3 gather_fusion
  10.6 0.5 gather.13
  11.1 0.1 broadcast_in_dim.32
  11.3 0.7 broadcast_select_fusion
  11.9 37.5 %all_to_all.25 = bf16[32,4,5120]{2,1,0:T(4,128)(2,1)S(1)} all-to-all(bf16[32,4,5120]{2,1,0:T(4,128)(2,1)S(1)} %broadcast_select_fusion), channel_id=1, replica_groups=mesh['groups'=2,'ep'=4,'tp'=2,'dp'=2] {'ep'}, dimensions={0} | all-to-all | bytes 2621440 | tf_op jit(solution)/shard_map/all_to_all | solution.py:42
  49.4 1.6 copy.13
  51.1 39.7 %all-gather.2.cloned.1.call-done = bf16[4,4,8,4,5120]{4,3,1,0,2:T(4,128)(2,1)} async-done(((bf16[1,4,8,4,5120]{4,3,1,0,2:T(4,128)(2,1)}), bf16[4,4,8,4,5120]{4,3,1,0,2:T(4,128)(2,1)}) %all-gather.2.cloned.1.call-update) | async-done | bytes 5242896 | tf_op jit(solution)/shard_map/all_gather | solution.py:44
  90.8 13.1 %fusion.31 = f32[4,4,8,4,256]{4,3,1,0,2:T(4,128)S(1)} fusion(bf16[4,4,8,4,5120]{4,3,1,0,2:T(4,128)(2,1)} %all-gather.2.cloned.1.call-done, bf16[8,5120,256]{2,1,0:T(8,128)(2,1)} %param.9), kind=kOutput, calls=%fused_computation.26 | convolution fusion | flops 1342177280 | bytes 26738688 | tf_op jit(solution)/shard_map/gsecd,edf->gsecf/dot_general | solution.py:45
  103.9 11.5 %fusion.40 = bf16[4,4,8,4,256]{4,3,1,0,2:T(4,128)(2,1)S(1)} fusion(bf16[4,4,8,4,5120]{4,3,1,0,2:T(4,128)(2,1)S(1)} %copy-done.4, bf16[8,5120,256]{2,1,0:T(8,128)(2,1)} %param.10, f32[4,4,8,4,256]{4,3,1,0,2:T(4,128)S(1)} %fusion.31), kind=kOutput, calls=%fused_computation.29 | convolution fusion | flops 1342963712 | bytes 27000832 | tf_op jit(solution)/shard_map/gsecd,edf->gsecf/dot_general | solution.py:46
  115.4 0.2 collective-permute-start
  115.6 5.0 %fusion.10 = f32[8,1280,4,4,4]{1,4,3,2,0:T(4,128)} fusion(bf16[4,4,8,4,256]{4,3,1,0,2:T(4,128)(2,1)S(1)} %fusion.40, bf16[8,1024,1280]{2,1,0:T(8,128)(2,1)} %param.11, s32[]{:T(128)S(6)} %select_n.65), kind=kOutput, calls=%fused_computation.13 | convolution fusion | flops 335544320 | bytes 8126468 | tf_op jit(solution)/shard_map/gsecf,efd->gsecd/dot_general | solution.py:52
  120.6 0.8 collective-permute-start.1
  121.4 6.7 %fusion.16 = f32[8,1280,4,4,4]{1,4,3,2,0:T(4,128)} fusion(f32[8,1280,4,4,4]{1,4,3,2,0:T(4,128)} %fusion.10, bf16[4,4,8,4,256]{4,3,1,0,2:T(4,128)(2,1)S(1)} %collective-permute-done, bf16[8,1024,1280]{2,1,0:T(8,128)(2,1)} %param.11, s32[]{:T(128)S(6)} %select_n.71), kind=kOutput, calls=%fused_computation.19 | convolution fusion | flops 336199680 | bytes 10747908 | tf_op jit(solution)/shard_map/gsecf,efd->gsecd/dot_general | solution.py:52
  128.1 1.3 collective-permute-start.2
  129.4 4.3 %fusion.19 = f32[8,1280,4,4,4]{1,4,3,2,0:T(4,128)} fusion(f32[8,1280,4,4,4]{1,4,3,2,0:T(4,128)} %fusion.16, bf16[4,4,8,4,256]{4,3,1,0,2:T(4,128)(2,1)S(1)} %collective-permute-done.1, bf16[8,1024,1280]{2,1,0:T(8,128)(2,1)S(1)} %bitcast.81, s32[]{:T(128)S(6)} %select_n.73), kind=kOutput, calls=%fused_computation.20 | convolution fusion | flops 336199680 | bytes 10747908 | tf_op jit(solution)/shard_map/gsecf,efd->gsecd/dot_general | solution.py:52
  133.7 2.8 %fusion.28 = bf16[4,4,8,4,1280]{4,3,1,0,2:T(4,128)(2,1)S(1)} fusion(f32[8,1280,4,4,4]{1,4,3,2,0:T(4,128)} %fusion.19, bf16[4,4,8,4,256]{4,3,1,0,2:T(4,128)(2,1)S(1)} %collective-permute-done.2, bf16[8,1024,1280]{2,1,0:T(8,128)(2,1)S(1)} %bitcast.81, s32[]{:T(128)S(6)} %select_n.75), kind=kOutput, calls=%fused_computation.23 | convolution fusion | flops 336855040 | bytes 9437188 | tf_op jit(solution)/shard_map/gsecf,efd->gsecd/dot_general | solution.py:52
  136.5 0.5 copy.14
  136.9 19.8 %all_to_all.26 = bf16[4,4,8,4,1280]{4,3,1,2,0:T(4,128)(2,1)S(1)} all-to-all(bf16[4,4,8,4,1280]{4,3,1,2,0:T(4,128)(2,1)S(1)} %copy.14), channel_id=1, replica_groups=mesh['groups'=2,'ep'=4,'tp'=2,'dp'=2] {'tp','dp'}, dimensions={0} | all-to-all | bytes 2621440 | tf_op jit(solution)/shard_map/all_to_all | solution.py:60
  156.7 1.0 copy.25
  157.7 1.4 reshape.111
  159.1 4.6 %all-to-all-start.2 = ((bf16[32,4,5120]{2,1,0:T(4,128)(2,1)}), bf16[32,4,5120]{2,1,0:T(4,128)(2,1)S(1)}, u32[]{:S(2)}, u32[]{:S(2)}) async-start(bf16[32,4,5120]{2,1,0:T(4,128)(2,1)} %reshape.111), calls=%async_computation.2 | async-start | bytes 2621440 | tf_op jit(solution)/shard_map/all_to_all | solution.py:62
  163.7 0.1 sub.15
  163.8 30.9 %all-to-all-done.2 = bf16[32,4,5120]{2,1,0:T(4,128)(2,1)S(1)} async-done(((bf16[32,4,5120]{2,1,0:T(4,128)(2,1)}), bf16[32,4,5120]{2,1,0:T(4,128)(2,1)S(1)}, u32[]{:S(2)}, u32[]{:S(2)}) %all-to-all-start.2) | async-done | bytes 1310752 | tf_op jit(solution)/shard_map/all_to_all | solution.py:62
  194.7 0.3 reshape.79
  195.0 0.9 gather_fusion.1
  196.0 1.2 multiply_reduce_fusion
  (35 shorter events, 0.2 us)
Async XLA Ops:
  6.5 2.8 %copy-start = (bf16[8,5120]{1,0:T(8,128)(2,1)S(1)}, bf16[8,5120]{1,0:T(8,128)(2,1)}, u32[]{:S(2)}) copy-start(bf16[8,5120]{1,0:T(8,128)(2,1)} %param.6) | copy-start | bytes 245764
  6.5 84.2 %all-gather.2.cloned.1.call-start = ((), (), s32[]{:S(2)}) async-start(), calls=%async_computation.3 | async-start | bytes 6553600 | tf_op jit(solution)/shard_map/all_gather | solution.py:44
  90.8 13.1 %copy-start.4 = (bf16[4,4,8,4,5120]{4,3,1,0,2:T(4,128)(2,1)S(1)}, bf16[4,4,8,4,5120]{4,3,1,0,2:T(4,128)(2,1)}, u32[]{:S(2)}) copy-start(bf16[4,4,8,4,5120]{4,3,1,0,2:T(4,128)(2,1)} %all-gather.2.cloned.1.call-done) | copy-start | bytes 15728644
  115.4 5.3 %collective-permute-start = (bf16[4,4,8,4,256]{4,3,1,0,2:T(4,128)(2,1)S(1)}, bf16[4,4,8,4,256]{4,3,1,0,2:T(4,128)(2,1)S(1)}, u32[]{:S(2)}, u32[]{:S(2)}) collective-permute-start(bf16[4,4,8,4,256]{4,3,1,0,2:T(4,128)(2,1)S(1)} %fusion.40), channel_id=1, source_target_pairs={{0,3},{1,0},{2,1},{3,2},{4,7},{5,4},{6,5},{7,6},{8,11},{9,8},{10,9... | collective-permute-start | bytes 786440 | tf_op jit(solution)/shard_map/ppermute | solution.py:16
  115.6 13.7 %slice-start = ((s8[20971520]{0:T(1024)(128)(4,1)}), s8[4194304]{0:T(1024)(128)(4,1)S(1)}, s32[]{:S(2)}) async-start(s8[20971520]{0:T(1024)(128)(4,1)} %bitcast.80), calls=%async_computation.4 | async-start | bytes 8388608
  115.6 13.7 %slice-start.1 = ((s8[20971520]{0:T(1024)(128)(4,1)}), s8[4194304]{0:T(1024)(128)(4,1)S(1)}, s32[]{:S(2)}) async-start(s8[20971520]{0:T(1024)(128)(4,1)} %bitcast.80), calls=%async_computation.5 | async-start | bytes 8388608
  115.6 13.7 %slice-start.2 = ((s8[20971520]{0:T(1024)(128)(4,1)}), s8[4194304]{0:T(1024)(128)(4,1)S(1)}, s32[]{:S(2)}) async-start(s8[20971520]{0:T(1024)(128)(4,1)} %bitcast.80), calls=%async_computation.6 | async-start | bytes 8388608
  120.6 8.7 %slice-start.3 = ((s8[20971520]{0:T(1024)(128)(4,1)}), s8[4194304]{0:T(1024)(128)(4,1)S(1)}, s32[]{:S(2)}) async-start(s8[20971520]{0:T(1024)(128)(4,1)} %bitcast.80), calls=%async_computation.7 | async-start | bytes 8388608
  120.6 8.7 %slice-start.4 = ((s8[20971520]{0:T(1024)(128)(4,1)}), s8[4194304]{0:T(1024)(128)(4,1)S(1)}, s32[]{:S(2)}) async-start(s8[20971520]{0:T(1024)(128)(4,1)} %bitcast.80), calls=%async_computation.8 | async-start | bytes 8388608
  120.6 7.4 %collective-permute-start.1 = (bf16[4,4,8,4,256]{4,3,1,0,2:T(4,128)(2,1)S(1)}, bf16[4,4,8,4,256]{4,3,1,0,2:T(4,128)(2,1)S(1)}, u32[]{:S(2)}, u32[]{:S(2)}) collective-permute-start(bf16[4,4,8,4,256]{4,3,1,0,2:T(4,128)(2,1)S(1)} %collective-permute-done), channel_id=1, source_target_pairs={{0,3},{1,0},{2,1},{3,2},{4,7},{5,4},{6,5},{7,6},{8,11},{9,8},{10,9... | collective-permute-start | bytes 786440 | tf_op jit(solution)/shard_map/ppermute | solution.py:16
  128.1 5.6 %collective-permute-start.2 = (bf16[4,4,8,4,256]{4,3,1,0,2:T(4,128)(2,1)S(1)}, bf16[4,4,8,4,256]{4,3,1,0,2:T(4,128)(2,1)S(1)}, u32[]{:S(2)}, u32[]{:S(2)}) collective-permute-start(bf16[4,4,8,4,256]{4,3,1,0,2:T(4,128)(2,1)S(1)} %collective-permute-done.1), channel_id=1, source_target_pairs={{0,3},{1,0},{2,1},{3,2},{4,7},{5,4},{6,5},{7,6},{8,11},{9,8},{10,9... | collective-permute-start | bytes 786440 | tf_op jit(solution)/shard_map/ppermute | solution.py:16
  157.7 6.1 %copy-start.2 = (s32[8,8]{1,0:T(8,128)S(1)}, s32[8,8]{1,0:T(8,128)}, u32[]{:S(2)}) copy-start(s32[8,8]{1,0:T(8,128)} %param.8) | copy-start | bytes 772
  159.1 35.6 %all-to-all-start.2 = ((bf16[32,4,5120]{2,1,0:T(4,128)(2,1)}), bf16[32,4,5120]{2,1,0:T(4,128)(2,1)S(1)}, u32[]{:S(2)}, u32[]{:S(2)}) async-start(bf16[32,4,5120]{2,1,0:T(4,128)(2,1)} %reshape.111), calls=%async_computation.2 | async-start | bytes 2621440 | tf_op jit(solution)/shard_map/all_to_all | solution.py:62
  194.7 2.5 %copy-start.1 = (bf16[8,5120]{1,0:T(8,128)(2,1)S(1)}, bf16[8,5120]{1,0:T(8,128)(2,1)}, u32[]{:S(2)}) copy-start(bf16[8,5120]{1,0:T(8,128)(2,1)} %param.6) | copy-start | bytes 245764
  195.0 0.9 copy-start.3
Sparse Core Ops, SparseCore 0:
  51.2 39.5 all-gather.1
